TPU v7x, 32 devices: a whole 2x2x4 slice. The times are simulated.
32 devices in a mesh: groups: 2 (over x), steps: 8 (over z, y), inner: 2 (over core).
Axes of the slice: x: 2, y: 2, z: 4, core: 2. Of those that a mesh axis runs over, the one named last changes fastest.
Arguments:
- start_state: float32 [16, 32, 768], P('groups'), parts along dimension 0, may hold values from -6 to 6
- noise_draws: float32 [32, 8, 32, 768], P(('groups', 'steps', 'inner')), parts along dimension 0, may hold values from -6 to 6
- step_gaps: int32 [32], P(('groups', 'steps', 'inner')), parts along dimension 0, may hold values from 1 to 15
- window_start: int32 [2], P('groups'), parts along dimension 0, may hold values from 240 to 999
- input_weight: bfloat16 [768, 1024], replicated, may hold values from -0.21875 to 0.21875
- embed_weight: bfloat16 [256, 2048], replicated, may hold values from -0.375 to 0.375
- first_weight: bfloat16 [1024, 1024], replicated, may hold values from -0.1875 to 0.1875
- second_weight: bfloat16 [1024, 1024], replicated, may hold values from -0.1875 to 0.1875
- output_weight: bfloat16 [1024, 768], replicated, may hold values from -0.1875 to 0.1875
Outputs:
- trajectory: float32 [32, 8, 32, 768], P(('groups', 'steps', 'inner')), parts along dimension 0
There are 2 independent parts, one for each index of `groups`. A program takes and returns all parts, laid end to end along the dimension named above; an argument that names none is the same for every part. Nothing has to cross between parts.
All inputs are finite; a program needn't handle non-finite values.
Results may differ from a plain program's by a relative error of at most 0.00035.
Values sent between devices are 32-bit elements; how exact they have to be, the bound alone decides.
A program may use at most 64 MiB of HBM per device.

v0:
```python
import functools
import math

import jax
import jax.numpy as jnp
import numpy as np
from jax import lax
from jax.experimental import pallas as pl
from jax.experimental.pallas import tpu as pltpu
from jax.sharding import PartitionSpec as P

GROUPS = 32
PIECES = 2
ITERS = 2
TRAIN_STEPS = 1000
CHUNK_IMAGES = 2
LANES = 128
BLOCK = 256
MESH = pl.DeviceIdType.MESH
F32 = jnp.float32
BF16 = jnp.bfloat16


def noise_table():
    levels = np.arange(TRAIN_STEPS, dtype=np.float32)
    beta = (0.0001 + (0.02 - 0.0001) * levels / (TRAIN_STEPS - 1)).astype(np.float32)
    bars = np.exp(np.cumsum(np.log1p(-beta.astype(np.float64)))).astype(np.float32)
    padded = np.zeros((-(-TRAIN_STEPS // (8 * LANES)) * 8 * LANES,), np.float32)
    padded[:TRAIN_STEPS] = bars
    return padded.reshape(-1, LANES)


def frequencies(count):
    powers = -math.log(10000.0) * np.arange(count, dtype=np.float32) / count
    return np.exp(powers.astype(np.float32)).astype(np.float32)[None, :]


def group_matrix(channels, rows):
    width = channels // GROUPS
    place = np.arange(BLOCK) // width
    same = (place[:, None] == place[None, :]).astype(np.float32)
    return same / (width * rows)


def silu(value):
    half = 0.5 * value
    return half + half * jnp.tanh(half)


def kernel(
    cfg,
    gap_ref,
    start_level_ref,
    table_ref,
    freq_ref,
    group_ref,
    start_hbm,
    noise_hbm,
    win_hbm,
    wemb_hbm,
    w1_hbm,
    w2_hbm,
    wout_hbm,
    out_v,
    start_v,
    noise_v,
    win,
    wemb,
    w1,
    w2,
    wout,
    gap_send,
    gap_all,
    modulation_v,
    coef_v,
    drift_v,
    core_rx,
    chain_rx,
    chain_tx,
    side_rx,
    final_tx,
    prefix_v,
    load_sem,
    gap_send_sem,
    gap_recv_sem,
    core_send,
    core_recv,
    chain_send,
    chain_recv,
    side_send,
    side_recv,
    final_send,
    final_recv,
):
    steps, inner, columns, chunks, size, patches, features, channels = cfg
    rows = steps // columns
    half = size // 2
    total = size * patches
    s = lax.axis_index("steps")
    h = lax.axis_index("inner")
    z, y = s // columns, lax.rem(s, columns)
    window = steps * inner
    me = s * inner + h
    messages = ITERS * chunks

    loads = [
        pltpu.make_async_copy(src, dst, load_sem.at[i])
        for i, (src, dst) in enumerate(
            [
                (start_hbm, start_v),
                (win_hbm, win),
                (wemb_hbm, wemb),
                (w1_hbm, w1),
                (w2_hbm, w2),
                (wout_hbm, wout),
                (noise_hbm, noise_v),
            ]
        )
    ]
    for load in loads:
        load.start()
    gap_send[...] = jnp.zeros_like(gap_send) + gap_ref[0]

    barrier = pltpu.get_barrier_semaphore()
    for j in range(1, window):
        to = lax.rem(me + j, window)
        pl.semaphore_signal(
            barrier,
            inc=1,
            device_id={"steps": to // inner, "inner": lax.rem(to, inner)},
            device_id_type=MESH,
        )
    pl.semaphore_wait(barrier, window - 1)

    def gap_copy(j):
        to = lax.rem(me + j, window)
        return pltpu.make_async_remote_copy(
            src_ref=gap_send,
            dst_ref=gap_all.at[me],
            send_sem=gap_send_sem.at[j],
            recv_sem=gap_recv_sem.at[me],
            device_id={"steps": to // inner, "inner": lax.rem(to, inner)},
            device_id_type=MESH,
        )

    def gap_arrival(j):
        origin = lax.rem(me + j, window)
        return pltpu.make_async_remote_copy(
            src_ref=gap_send,
            dst_ref=gap_all.at[origin],
            send_sem=gap_send_sem.at[j],
            recv_sem=gap_recv_sem.at[origin],
            device_id={"steps": origin // inner, "inner": lax.rem(origin, inner)},
            device_id_type=MESH,
        )

    for j in range(1, window):
        gap_copy(j).start()

    for n in range(chunks):
        prefix_v[n] = jnp.zeros(prefix_v.shape[1:], F32)

    @pl.when(z == 0)
    def _():
        chain_rx[...] = jnp.zeros_like(chain_rx)

    def core_copy(m):
        return pltpu.make_async_remote_copy(
            src_ref=drift_v.at[m, 1 - h],
            dst_ref=core_rx.at[m],
            send_sem=core_send.at[m],
            recv_sem=core_recv.at[m],
            device_id={"inner": 1 - h},
            device_id_type=MESH,
        )

    depth = patches // PIECES

    def part(ref, m, q):
        return ref.at[m, :, q * depth : (q + 1) * depth]

    def chain_copy(m, q):
        return pltpu.make_async_remote_copy(
            src_ref=part(chain_tx, m, q),
            dst_ref=part(chain_rx, m, q),
            send_sem=chain_send.at[m, q],
            recv_sem=chain_recv.at[m, q],
            device_id={"steps": lax.rem(s + columns, steps)},
            device_id_type=MESH,
        )

    def side_copy(m, source, q):
        return pltpu.make_async_remote_copy(
            src_ref=part(source, m, q),
            dst_ref=part(side_rx, m, q),
            send_sem=side_send.at[m, q],
            recv_sem=side_recv.at[m, q],
            device_id={"steps": z * columns + (1 - y)},
            device_id_type=MESH,
        )

    def final_copy(m):
        return pltpu.make_async_remote_copy(
            src_ref=final_tx.at[m],
            dst_ref=prefix_v.at[m + chunks, h],
            send_sem=final_send.at[m],
            recv_sem=final_recv.at[m],
            device_id={"inner": 1 - h},
            device_id_type=MESH,
        )

    def final_arrival(m):
        return pltpu.make_async_remote_copy(
            src_ref=final_tx.at[m],
            dst_ref=prefix_v.at[m + chunks, 1 - h],
            send_sem=final_send.at[m],
            recv_sem=final_recv.at[m],
            device_id={"inner": 1 - h},
            device_id_type=MESH,
        )

    def chain(m):
        core_copy(m).wait_recv()
        for q in range(PIECES):
            cut = slice(q * depth, (q + 1) * depth)

            @pl.when(z > 0)
            def _():
                chain_copy(m, q).wait_recv()

            chain_tx[m, :, cut] = chain_rx[m, :, cut] + (drift_v[m, h, :, cut] + core_rx[m, :, cut])

            @pl.when(z < rows - 1)
            def _():
                chain_copy(m, q).start()

            if columns == 2:

                @pl.when(y == 0)
                def _():
                    side_copy(m, chain_tx, q).start()

                @pl.when(y == 1)
                def _():
                    side_copy(m, chain_rx, q).start()

    def hand_back(m):
        prefix = chain_rx[m]
        if columns == 2:
            for q in range(PIECES):
                side_copy(m, chain_tx, q).wait_recv()
            prefix = prefix + side_rx[m]

        @pl.when(h == 0)
        def _():
            final_tx[m] = prefix + drift_v[m, 0]
            prefix_v[m + chunks, 0] = prefix

        @pl.when(h == 1)
        def _():
            final_tx[m] = prefix
            prefix_v[m + chunks, 1] = prefix + core_rx[m]

        final_copy(m).start()

    def finish(m):
        final_arrival(m).wait_recv()

    def group_average(partial):
        blocks = channels // BLOCK
        stacked = jnp.concatenate(
            [partial[:, i * BLOCK : (i + 1) * BLOCK] for i in range(blocks)], axis=0
        )
        matrix = group_ref[...]
        high = stacked.astype(BF16)
        rest = stacked - high.astype(F32)
        middle = rest.astype(BF16)
        low = (rest - middle.astype(F32)).astype(BF16)
        parts = jnp.concatenate([low, middle, high], axis=0)
        summed = jnp.dot(parts, matrix, preferred_element_type=F32)
        summed = jnp.sum(summed.reshape(3, -1, BLOCK), axis=0)
        summed = jnp.sum(summed.reshape(blocks, size, 8, BLOCK), axis=2, keepdims=True)
        return jnp.concatenate([summed[i] for i in range(blocks)], axis=-1)

    def row_sums(value):
        return jnp.sum(value.reshape(size, patches // 8, 8, channels), axis=1).reshape(
            size * 8, channels
        )

    def centered(hidden):
        shaped = hidden.reshape(size, patches, channels)
        offset = shaped - group_average(row_sums(shaped))
        return offset, lax.rsqrt(group_average(row_sums(offset * offset)) + 1e-05)

    def set_level():
        for j in range(1, window):
            gap_arrival(j).wait_recv()
        earlier = jnp.zeros(gap_send.shape, jnp.int32)
        for k in range(window):
            earlier = earlier + jnp.where(k < me, gap_all[k], 0)
        level_now = start_level_ref[0] - earlier
        level_next = level_now - gap_ref[0]
        table = table_ref[...]
        places = lax.broadcasted_iota(jnp.int32, table.shape, 0) * LANES + (
            lax.broadcasted_iota(jnp.int32, table.shape, 1)
        )

        def lookup(level):
            found = jnp.where(places == level[:1, :1], table, 0.0)
            return jnp.sum(jnp.sum(found, axis=0, keepdims=True), axis=1, keepdims=True)

        bar_now, bar_next = lookup(level_now), lookup(level_next)
        coefs = [
            jnp.sqrt(1.0 - bar_now),
            1.0 / jnp.sqrt(bar_now),
            jnp.sqrt(bar_now),
            1.0 / jnp.sqrt(1.0 - bar_now),
            jnp.sqrt(bar_next),
            (1.0 - bar_next) * jnp.sqrt(bar_now / (bar_next * (1.0 - bar_now))),
            jnp.sqrt((1.0 - bar_next) / (1.0 - bar_now) * (1.0 - bar_now / bar_next)),
        ]
        for i, coef in enumerate(coefs):
            coef_v[i] = jnp.broadcast_to(coef, coef_v.shape[1:])
        angles = level_now.astype(F32)[:, :1] * freq_ref[...]
        around = jnp.concatenate([jnp.cos(angles), jnp.sin(angles)], axis=1).astype(BF16)
        loads[2].wait()
        modulation_v[...] = jnp.dot(around, wemb[...], preferred_element_type=F32)

    def compute(n):
        c = lax.rem(n, chunks)

        state = start_v[c] + prefix_v[n].reshape(size, patches, features)
        flat = state.reshape(total, features).astype(BF16)
        entry = jnp.dot(flat, win[...], preferred_element_type=F32)
        offset, spread = centered(entry)

        scale = modulation_v[:1, :channels].reshape(1, 1, channels)
        shift = modulation_v[:1, channels:].reshape(1, 1, channels)
        one = silu(offset * (spread * (1.0 + scale)) + shift).astype(BF16)
        middle = jnp.dot(one.reshape(total, channels), w1[...], preferred_element_type=F32)
        offset, spread = centered(middle)
        two = silu(offset * spread).astype(BF16)

        @pl.when(n >= chunks - 1)
        def _():
            hand_back(n - chunks + 1)

        block = entry + jnp.dot(
            two.reshape(total, channels), w2[...], preferred_element_type=F32
        )
        offset, spread = centered(block)
        three = silu(offset * spread).astype(BF16)

        eps = jnp.dot(three.reshape(total, channels), wout[...], preferred_element_type=F32)
        eps = eps.reshape(size, patches, features)
        state = start_v[c] + prefix_v[n].reshape(size, patches, features)
        coef = [coef_v[i][:1, :1].reshape(1, 1, 1) for i in range(7)]
        clean = jnp.clip((state - coef[0] * eps) * coef[1], -1.0, 1.0)
        implied = (state - coef[2] * clean) * coef[3]
        drift = coef[4] * clean + coef[5] * implied + coef[6] * noise_v[c] - state
        drift_v[n] = drift.reshape(2, half, patches, features)
        core_copy(n).start()

    def step(n, carry):
        @pl.when(n >= chunks)
        def _():
            finish(n - chunks)

        compute(n)

        @pl.when(n >= 1)
        def _():
            chain(n - 1)

        return carry

    for i in (0, 1, 3, 4, 5, 6):
        loads[i].wait()
    set_level()
    lax.fori_loop(0, messages, step, 0)

    def emit(m):
        finish(m)
        c = m - (ITERS - 1) * chunks
        whole = prefix_v[m + chunks] + drift_v[m]
        out_v[c] = start_v[c] + whole.reshape(size, patches, features)

    chain(messages - 1)
    for m in range(messages - chunks + 1, messages):
        hand_back(m)
        emit(m - 1)
    emit(messages - 1)

    for j in range(1, window):
        gap_copy(j).wait_send()
    for m in range(messages):
        core_copy(m).wait_send()
        final_copy(m).wait_send()
        if columns == 2:
            for q in range(PIECES):
                side_copy(m, chain_tx, q).wait_send()

    @pl.when(z < rows - 1)
    def _():
        for m in range(messages):
            for q in range(PIECES):
                chain_copy(m, q).wait_send()


def shards(
    steps,
    inner,
    start_state,
    noise_draws,
    step_gaps,
    window_start,
    input_weight,
    embed_weight,
    first_weight,
    second_weight,
    output_weight,
):
    batch, patches, features = start_state.shape
    channels = input_weight.shape[1]
    size = CHUNK_IMAGES
    half, chunks = size // 2, batch // size
    columns = 2 if steps % 2 == 0 else 1
    window = steps * inner
    messages = ITERS * chunks
    chunked = (chunks, size, patches, features)
    piece = (messages, half, patches, features)
    cfg = (steps, inner, columns, chunks, size, patches, features, channels)
    table = jnp.asarray(noise_table())
    freq = jnp.asarray(frequencies(embed_weight.shape[0] // 2))
    matrix = jnp.asarray(group_matrix(channels, patches)).astype(BF16)
    smem = pl.BlockSpec(memory_space=pltpu.SMEM)
    vmem = pl.BlockSpec(memory_space=pltpu.VMEM)
    anywhere = pl.BlockSpec(memory_space=pltpu.HBM)
    dma = pltpu.SemaphoreType.DMA
    out = pl.pallas_call(
        functools.partial(kernel, cfg),
        out_shape=pltpu.VMEM(chunked, F32),
        in_specs=[smem, smem, vmem, vmem, vmem] + [anywhere] * 7,
        out_specs=vmem,
        scratch_shapes=[
            pltpu.VMEM(chunked, F32),
            pltpu.VMEM(chunked, F32),
            pltpu.VMEM(input_weight.shape, BF16),
            pltpu.VMEM(embed_weight.shape, BF16),
            pltpu.VMEM(first_weight.shape, BF16),
            pltpu.VMEM(second_weight.shape, BF16),
            pltpu.VMEM(output_weight.shape, BF16),
            pltpu.VMEM((8, LANES), jnp.int32),
            pltpu.VMEM((window, 8, LANES), jnp.int32),
            pltpu.VMEM((8, 2 * channels), F32),
            pltpu.VMEM((7, 8, LANES), F32),
            pltpu.VMEM((messages, 2, half, patches, features), F32),
            pltpu.VMEM(piece, F32),
            pltpu.VMEM(piece, F32),
            pltpu.VMEM(piece, F32),
            pltpu.VMEM(piece, F32),
            pltpu.VMEM(piece, F32),
            pltpu.VMEM((messages + chunks, 2, half, patches, features), F32),
            dma((7,)),
            dma((window,)),
            dma((window,)),
        ]
        + [dma((messages,))] * 2
        + [dma((messages, PIECES))] * 4
        + [dma((messages,))] * 2,
        compiler_params=pltpu.CompilerParams(
            collective_id=0, has_side_effects=True, vmem_limit_bytes=56 * 1024 * 1024
        ),
    )(
        step_gaps,
        window_start,
        table,
        freq,
        matrix,
        start_state.reshape(chunked),
        noise_draws.reshape(chunked),
        input_weight,
        embed_weight,
        first_weight,
        second_weight,
        output_weight,
    )
    return out.reshape((1,) + start_state.shape)


def solution(mesh):
    steps, inner = mesh.shape["steps"], mesh.shape["inner"]
    return jax.shard_map(
        functools.partial(shards, steps, inner),
        mesh=mesh,
        in_specs=(
            P("groups", None, None),
            P(("groups", "steps", "inner"), None, None, None),
            P(("groups", "steps", "inner")),
            P("groups"),
            P(),
            P(),
            P(),
            P(),
            P(),
        ),
        out_specs=P(("groups", "steps", "inner"), None, None, None),
        check_vma=False,
    )
```

profile of v0, /device:TPU:25, one launch (start us, length us, event | category | flops | bytes accessed | tf_op | source)
XLA Modules:
  0.0 54.2 jit_solution(5047134572387963194)
XLA Ops:
  1.3 52.0 %shard_map.118 = f32[4,2,32,768]{3,2,1,0:T(8,128)S(1)} custom-call(s32[1]{0:T(128)S(6)} %copy.15.gap_ref, s32[1]{0:T(128)S(6)} %copy.16.start_level_ref, f32[8,128]{1,0:T(8,128)} %constant.6.clone.table_ref, f32[1,128]{1,0:T(1,128)} %constant.7.clone.freq_ref, bf16[256,256]{1,0:T(8,128)(2,1)} %constant.12.group_ref, f32[4,2,32,768]{3,2,1,0:T(8,128)} %bitcast.4, ...), custom_call_target="tpu_custom_call" | custom-call | tf_op jit(solution)/shard_map/pallas_call | solution.py:440
  53.3 0.9 %copy.14 = f32[1,8,32,768]{3,2,1,0:T(8,128)} copy(f32[1,8,32,768]{3,2,1,0:T(8,128)S(1)} %bitcast.3) | data formatting | bytes 1572864
where the time goes:
time: 54.3 us; the launch traced here: 54.2 us
  Pallas kernels  52 us (96%)
  between operations  1.3 us (2%)
  local copies, waits for them, and re-layouts  0.88 us (2%)
    pallas_call x1, Pallas kernels, shards(): pl.pallas_call(functools.partial(kernel, cfg), out_shape=pltpu.VMEM(chunk...  52 us

commit v1 on v0

v1 whole, which is shorter than its diff:
```python
import functools
import math

import jax
import jax.numpy as jnp
import numpy as np
from jax import lax
from jax.experimental import pallas as pl
from jax.experimental.pallas import tpu as pltpu
from jax.sharding import PartitionSpec as P

GROUPS = 32
PIECES = 2
FIRST = ((0, 1),)
SECOND = ((0,), (1,))
ITERS = 2
TRAIN_STEPS = 1000
LANES = 128
BLOCK = 256
MESH = pl.DeviceIdType.MESH
F32 = jnp.float32
BF16 = jnp.bfloat16


def noise_table():
    levels = np.arange(TRAIN_STEPS, dtype=np.float32)
    beta = (0.0001 + (0.02 - 0.0001) * levels / (TRAIN_STEPS - 1)).astype(np.float32)
    bars = np.exp(np.cumsum(np.log1p(-beta.astype(np.float64)))).astype(np.float32)
    padded = np.zeros((-(-TRAIN_STEPS // (8 * LANES)) * 8 * LANES,), np.float32)
    padded[:TRAIN_STEPS] = bars
    return padded.reshape(-1, LANES)


def frequencies(count):
    powers = -math.log(10000.0) * np.arange(count, dtype=np.float32) / count
    return np.exp(powers.astype(np.float32)).astype(np.float32)[None, :]


def group_matrix(channels, rows):
    width = channels // GROUPS
    place = np.arange(BLOCK) // width
    same = (place[:, None] == place[None, :]).astype(np.float32)
    return same / (width * rows)


def silu(value):
    half = 0.5 * value
    return half + half * jnp.tanh(half)


def kernel(
    cfg,
    gap_ref,
    start_level_ref,
    table_ref,
    freq_ref,
    group_ref,
    start_hbm,
    noise_hbm,
    win_hbm,
    wemb_hbm,
    w1_hbm,
    w2_hbm,
    wout_hbm,
    out_v,
    start_v,
    noise_v,
    noise_all,
    win,
    wemb,
    w1,
    w2,
    wout,
    gap_send,
    gap_all,
    base_rx,
    base_tx,
    modulation_v,
    coef_v,
    part_v,
    state_v,
    chain_rx,
    chain_tx,
    out_tx,
    load_sem,
    gap_send_sem,
    gap_recv_sem,
    base_sem,
    noise_send,
    noise_recv,
    chain_send,
    chain_recv,
    out_send,
    out_recv,
):
    steps, inner, columns, own, patches, features, channels = cfg
    rows = steps // columns
    plane = columns * inner
    s = lax.axis_index("steps")
    h = lax.axis_index("inner")
    z = s // columns
    p = lax.rem(s, columns) * inner + h
    first = p * own

    def load(i, src, dst):
        return pltpu.make_async_copy(src, dst, load_sem.at[i])

    loads = [
        load(0, noise_hbm, noise_v),
        load(1, start_hbm.at[pl.ds(first, own)], start_v),
        load(2, win_hbm, win),
        load(3, noise_hbm.at[pl.ds(first, own)], noise_all.at[p]),
        load(4, wemb_hbm, wemb),
        load(5, w1_hbm, w1),
        load(6, w2_hbm, w2),
        load(7, wout_hbm, wout),
    ]
    for copy in loads:
        copy.start()

    def mate(r):
        q = lax.rem(p + r, plane)
        return q, {"steps": z * columns + q // inner, "inner": lax.rem(q, inner)}

    below, above = {"steps": s - columns}, {"steps": s + columns}

    barrier = pltpu.get_barrier_semaphore()
    for r in range(1, plane):
        pl.semaphore_signal(barrier, inc=1, device_id=mate(r)[1], device_id_type=MESH)

    @pl.when(z > 0)
    def _():
        pl.semaphore_signal(barrier, inc=1, device_id=below, device_id_type=MESH)

    @pl.when(z < rows - 1)
    def _():
        pl.semaphore_signal(barrier, inc=1, device_id=above, device_id_type=MESH)

    gap_send[...] = jnp.zeros_like(gap_send) + gap_ref[0]
    gap_all[p] = jnp.zeros_like(gap_send) + gap_ref[0]

    @pl.when(z == 0)
    def _():
        base_rx[...] = jnp.zeros_like(base_rx)
        chain_rx[...] = jnp.zeros_like(chain_rx)

    neighbours = (z + rows - 1) // rows + (2 * rows - 2 - z) // rows
    pl.semaphore_wait(barrier, plane - 1 + neighbours)

    def gap_copy(r, slot):
        return pltpu.make_async_remote_copy(
            src_ref=gap_send,
            dst_ref=gap_all.at[slot],
            send_sem=gap_send_sem.at[r],
            recv_sem=gap_recv_sem.at[slot],
            device_id=mate(r)[1],
            device_id_type=MESH,
        )

    def base_copy():
        return pltpu.make_async_remote_copy(
            src_ref=base_tx,
            dst_ref=base_rx,
            send_sem=base_sem.at[0],
            recv_sem=base_sem.at[1],
            device_id=above,
            device_id_type=MESH,
        )

    def noise_copy(j, r, slot):
        q, device = mate(r)
        return pltpu.make_async_remote_copy(
            src_ref=noise_v.at[q * own + j],
            dst_ref=noise_all.at[slot, j],
            send_sem=noise_send.at[j, r],
            recv_sem=noise_recv.at[slot, j],
            device_id=device,
            device_id_type=MESH,
        )

    def out_copy(j, r, slot):
        q, device = mate(r)
        return pltpu.make_async_remote_copy(
            src_ref=out_tx.at[j, q],
            dst_ref=out_v.at[slot * own + j],
            send_sem=out_send.at[j, r],
            recv_sem=out_recv.at[slot, j],
            device_id=device,
            device_id_type=MESH,
        )

    depth = patches // PIECES

    def chain_copy(n, j, q):
        cut = pl.ds(q * depth, depth)
        return pltpu.make_async_remote_copy(
            src_ref=chain_tx.at[n, j, cut],
            dst_ref=chain_rx.at[n, j, cut],
            send_sem=chain_send.at[n, j, q],
            recv_sem=chain_recv.at[n, j, q],
            device_id=above,
            device_id_type=MESH,
        )

    for r in range(1, plane):
        gap_copy(r, p).start()
    loads[0].wait()
    for j in range(own):
        for r in range(1, plane):
            noise_copy(j, r, p).start()

    def group_average(partial, size):
        blocks = channels // BLOCK
        stacked = jnp.concatenate(
            [partial[:, i * BLOCK : (i + 1) * BLOCK] for i in range(blocks)], axis=0
        )
        matrix = group_ref[...]
        high = stacked.astype(BF16)
        rest = stacked - high.astype(F32)
        middle = rest.astype(BF16)
        low = (rest - middle.astype(F32)).astype(BF16)
        parts = jnp.concatenate([low, middle, high], axis=0)
        summed = jnp.dot(parts, matrix, preferred_element_type=F32)
        summed = jnp.sum(summed.reshape(3, -1, BLOCK), axis=0)
        summed = jnp.sum(summed.reshape(blocks, size, 8, BLOCK), axis=2, keepdims=True)
        return jnp.concatenate([summed[i] for i in range(blocks)], axis=-1)

    def row_sums(value, size):
        return jnp.sum(value.reshape(size, patches // 8, 8, channels), axis=1).reshape(
            size * 8, channels
        )

    def centered(hidden, size):
        shaped = hidden.reshape(size, patches, channels)
        offset = shaped - group_average(row_sums(shaped, size), size)
        return offset, lax.rsqrt(group_average(row_sums(offset * offset, size), size) + 1e-05)

    def project(value, weight):
        return jnp.dot(value, weight[...], preferred_element_type=F32)

    def set_levels():
        for r in range(1, plane):
            slot = mate(r)[0]
            gap_copy(r, slot).wait_recv()

        @pl.when(z > 0)
        def _():
            base_copy().wait_recv()

        gaps = [gap_all[t] for t in range(plane)]
        base = base_rx[...]
        total = base
        for gap in gaps:
            total = total + gap
        base_tx[...] = total

        @pl.when(z < rows - 1)
        def _():
            base_copy().start()

        table = table_ref[...]
        tall = lax.broadcasted_iota(jnp.int32, table.shape, 0)
        places = tall * LANES + lax.broadcasted_iota(jnp.int32, table.shape, 1)
        level = start_level_ref[0] - base
        levels = [level]
        for gap in gaps:
            level = level - gap
            levels.append(level)

        def lookup(level):
            found = jnp.where(places == level[:1, :1], table, 0.0)
            return jnp.sum(jnp.sum(found, axis=0, keepdims=True), axis=1, keepdims=True)

        bars = [lookup(level) for level in levels]
        bar_now, bar_next = jnp.ones(table.shape, F32), jnp.ones(table.shape, F32)
        level_now = levels[0]
        for t in range(plane):
            bar_now = jnp.where(tall == t, bars[t], bar_now)
            bar_next = jnp.where(tall == t, bars[t + 1], bar_next)
            level_now = jnp.where(tall == t, levels[t], level_now)
        coefs = [
            jnp.sqrt(1.0 - bar_now),
            1.0 / jnp.sqrt(bar_now),
            jnp.sqrt(bar_now),
            1.0 / jnp.sqrt(1.0 - bar_now),
            jnp.sqrt(bar_next),
            (1.0 - bar_next) * jnp.sqrt(bar_now / (bar_next * (1.0 - bar_now))),
            jnp.sqrt((1.0 - bar_next) / (1.0 - bar_now) * (1.0 - bar_now / bar_next)),
        ]
        for i, coef in enumerate(coefs):
            coef_v[i] = coef
        angles = level_now.astype(F32) * freq_ref[...]
        around = jnp.concatenate([jnp.cos(angles), jnp.sin(angles)], axis=1).astype(BF16)
        loads[4].wait()
        modulation_v[...] = project(around, wemb)

    def modulations(low):
        return jnp.concatenate(
            [modulation_v[t : t + 1, low : low + channels] for t in range(plane)], axis=0
        ).reshape(plane, 1, channels)

    def drifts(n, j, eps):
        result = []
        for t in range(plane):
            state = start_v[j] if n == 0 else state_v[j, t]
            coef = [coef_v[i][t : t + 1, :1] for i in range(7)]
            clean = jnp.clip((state - coef[0] * eps[t]) * coef[1], -1.0, 1.0)
            implied = (state - coef[2] * clean) * coef[3]
            result.append(coef[4] * clean + coef[5] * implied + coef[6] * noise_all[t, j] - state)
        return result

    def forward(n, j):
        for q in range(PIECES):
            cut = pl.ds(q * depth, depth)
            chain_copy(n, j, q).wait_recv()
            chain_tx[n, j, cut] = chain_tx[n, j, cut] + chain_rx[n, j, cut]

            @pl.when(z < rows - 1)
            def _():
                chain_copy(n, j, q).start()

    def launch(n, j):
        for q in range(PIECES):
            chain_copy(n, j, q).start()

    def denoise(n, group, entries, entry_norms, between):
        scale, shift = 1.0 + modulations(0), modulations(channels)
        ones = []
        for offset, spread in entry_norms:
            ones.append(silu(offset * (spread * scale) + shift).astype(BF16))
        if n == 0:
            loads[5].wait()
        middles = [project(one.reshape(-1, channels), w1) for one in ones]
        twos = []
        for middle in middles:
            offset, spread = centered(middle, plane)
            twos.append(silu(offset * spread).astype(BF16))
        if n == 0:
            loads[6].wait()
        blocks = []
        for entry, two in zip(entries, twos):
            added = project(two.reshape(-1, channels), w2).reshape(plane, patches, channels)
            blocks.append(entry + added)
        threes = []
        for block in blocks:
            offset, spread = centered(block, plane)
            threes.append(silu(offset * spread).astype(BF16))
        if n == 0:
            loads[7].wait()
        for j, three in zip(group, threes):
            eps = project(three.reshape(-1, channels), wout).reshape(plane, patches, features)
            between(j)
            finish(n, j, eps)

    def finish(n, j, eps):
        steps_of = drifts(n, j, eps)
        running = steps_of[0]
        if n == 0:
            for t in range(1, plane):
                part_v[j, t] = running
                running = running + steps_of[t]
            chain_tx[n, j] = running

            @pl.when(z == 0)
            def _():
                launch(n, j)
        else:
            origin = start_v[j]
            out_tx[j, 0] = origin + running
            for t in range(1, plane):
                running = running + steps_of[t]
                out_tx[j, t] = origin + running
            chain_tx[n, j] = running

            @pl.when(z == 0)
            def _():
                launch(n, j)

            @pl.when(z > 0)
            def _():
                forward(n, j)
                earlier = chain_rx[n, j]
                for t in range(plane):
                    out_tx[j, t] = out_tx[j, t] + earlier

            for r in range(1, plane):
                out_copy(j, r, p).start()
            out_v[first + j] = out_tx[j, p]

    loads[1].wait()
    loads[2].wait()
    flat = start_v[...].reshape(own * patches, features).astype(BF16)
    entry = project(flat, win)
    offset, spread = centered(entry, own)
    shaped = entry.reshape(own, patches, channels)
    set_levels()

    def noise_arrives(j):
        if j == 0:
            loads[3].wait()
        for r in range(1, plane):
            slot = mate(r)[0]
            noise_copy(j, r, slot).wait_recv()

    for group in FIRST:
        denoise(
            0,
            group,
            [shaped[j : j + 1] for j in group],
            [(offset[j : j + 1], spread[j : j + 1]) for j in group],
            noise_arrives,
        )

    @pl.when(z > 0)
    def _():
        for j in range(own):
            forward(0, j)

    for group in SECOND:
        entries, norms = [], []
        for j in group:
            state_v[j, 0] = start_v[j] + chain_rx[0, j]
            for t in range(1, plane):
                state_v[j, t] = start_v[j] + (chain_rx[0, j] + part_v[j, t])
            flat = state_v[j].reshape(plane * patches, features).astype(BF16)
            entry = project(flat, win)
            entries.append(entry.reshape(plane, patches, channels))
            norms.append(centered(entry, plane))
        denoise(1, group, entries, norms, lambda j: None)

    for r in range(1, plane):
        slot = mate(r)[0]
        for j in range(own):
            out_copy(j, r, slot).wait_recv()

    for r in range(1, plane):
        gap_copy(r, p).wait_send()
        for j in range(own):
            noise_copy(j, r, p).wait_send()
            out_copy(j, r, p).wait_send()

    @pl.when(z < rows - 1)
    def _():
        base_copy().wait_send()
        for n in range(ITERS):
            for j in range(own):
                for q in range(PIECES):
                    chain_copy(n, j, q).wait_send()


def shards(
    steps,
    inner,
    start_state,
    noise_draws,
    step_gaps,
    window_start,
    input_weight,
    embed_weight,
    first_weight,
    second_weight,
    output_weight,
):
    batch, patches, features = start_state.shape
    channels = input_weight.shape[1]
    columns = 2 if steps % 2 == 0 else 1
    plane = columns * inner
    own = batch // plane
    cfg = (steps, inner, columns, own, patches, features, channels)
    image = (patches, features)
    table = jnp.asarray(noise_table())
    freq = jnp.asarray(frequencies(embed_weight.shape[0] // 2))
    matrix = jnp.asarray(group_matrix(channels, patches)).astype(BF16)
    smem = pl.BlockSpec(memory_space=pltpu.SMEM)
    vmem = pl.BlockSpec(memory_space=pltpu.VMEM)
    anywhere = pl.BlockSpec(memory_space=pltpu.HBM)
    dma = pltpu.SemaphoreType.DMA
    out = pl.pallas_call(
        functools.partial(kernel, cfg),
        out_shape=pltpu.VMEM((batch,) + image, F32),
        in_specs=[smem, smem, vmem, vmem, vmem] + [anywhere] * 7,
        out_specs=vmem,
        scratch_shapes=[
            pltpu.VMEM((own,) + image, F32),
            pltpu.VMEM((batch,) + image, F32),
            pltpu.VMEM((plane, own) + image, F32),
            pltpu.VMEM(input_weight.shape, BF16),
            pltpu.VMEM(embed_weight.shape, BF16),
            pltpu.VMEM(first_weight.shape, BF16),
            pltpu.VMEM(second_weight.shape, BF16),
            pltpu.VMEM(output_weight.shape, BF16),
            pltpu.VMEM((8, LANES), jnp.int32),
            pltpu.VMEM((plane, 8, LANES), jnp.int32),
            pltpu.VMEM((8, LANES), jnp.int32),
            pltpu.VMEM((8, LANES), jnp.int32),
            pltpu.VMEM((8, 2 * channels), F32),
            pltpu.VMEM((7, 8, LANES), F32),
            pltpu.VMEM((own, plane) + image, F32),
            pltpu.VMEM((own, plane) + image, F32),
            pltpu.VMEM((ITERS, own) + image, F32),
            pltpu.VMEM((ITERS, own) + image, F32),
            pltpu.VMEM((own, plane) + image, F32),
            dma((8,)),
            dma((plane,)),
            dma((plane,)),
            dma((2,)),
            dma((own, plane)),
            dma((plane, own)),
            dma((ITERS, own, PIECES)),
            dma((ITERS, own, PIECES)),
            dma((own, plane)),
            dma((plane, own)),
        ],
        compiler_params=pltpu.CompilerParams(
            collective_id=0, has_side_effects=True, vmem_limit_bytes=56 * 1024 * 1024
        ),
    )(
        step_gaps,
        window_start,
        table,
        freq,
        matrix,
        start_state,
        noise_draws.reshape((batch,) + image),
        input_weight,
        embed_weight,
        first_weight,
        second_weight,
        output_weight,
    )
    return out.reshape((1,) + start_state.shape)


def solution(mesh):
    steps, inner = mesh.shape["steps"], mesh.shape["inner"]
    return jax.shard_map(
        functools.partial(shards, steps, inner),
        mesh=mesh,
        in_specs=(
            P("groups", None, None),
            P(("groups", "steps", "inner"), None, None, None),
            P(("groups", "steps", "inner")),
            P("groups"),
            P(),
            P(),
            P(),
            P(),
            P(),
        ),
        out_specs=P(("groups", "steps", "inner"), None, None, None),
        check_vma=False,
    )
```

time: 54.3 us -> 38 us (0.70)
  Pallas kernels: 52 us -> 35.7 us
    pallas_call x1, Pallas kernels: 52 us -> 35.7 us  [shards(): pl.pallas_call(functools.partial(kernel, cfg), out_shape=pltpu.VMEM((batc...]
where the time goes in v1:
time: 38 us; the launch traced here: 37.8 us
  Pallas kernels  35.7 us (94%)
  between operations  1.3 us (3%)
  local copies, waits for them, and re-layouts  0.88 us (2%)
    pallas_call x1, Pallas kernels, shards(): pl.pallas_call(functools.partial(kernel, cfg), out_shape=pltpu.VMEM((batc...  35.7 us
    unnamed x1, local copies, waits for them, and re-layouts  0.88 us

profile of v1, /device:TPU:25, one launch (start us, length us, event | category | flops | bytes accessed | tf_op | source)
XLA Modules:
  0.0 37.8 jit_solution(6333408452977617427)
XLA Ops:
  1.3 35.7 %shard_map.118 = f32[8,32,768]{2,1,0:T(8,128)S(1)} custom-call(s32[1]{0:T(128)S(6)} %copy.15.gap_ref, s32[1]{0:T(128)S(6)} %copy.16.start_level_ref, f32[8,128]{1,0:T(8,128)} %constant.6.clone.table_ref, f32[1,128]{1,0:T(1,128)} %constant.7.clone.freq_ref, bf16[256,256]{1,0:T(8,128)(2,1)} %constant.12.group_ref, f32[8,32,768]{2,1,0:T(8,128)} %start_hbm.1, ...), custom_call_target="tpu_custom_call" | custom-call | tf_op jit(solution)/shard_map/pallas_call | solution.py:478
  37.0 0.9 %copy.14 = f32[1,8,32,768]{3,2,1,0:T(8,128)} copy(f32[1,8,32,768]{3,2,1,0:T(8,128)S(1)} %bitcast.2) | data formatting | bytes 1572864

commit v2 on v1

v2 whole, which is shorter than its diff:
```python
import functools
import math

import jax
import jax.numpy as jnp
import numpy as np
from jax import lax
from jax.experimental import pallas as pl
from jax.experimental.pallas import tpu as pltpu
from jax.sharding import PartitionSpec as P

GROUPS = 32
PIECES = 4
OUTER_ONE = False
OUTER_TWO = False
ITERS = 2
TRAIN_STEPS = 1000
LANES = 128
BLOCK = 256
MESH = pl.DeviceIdType.MESH
F32 = jnp.float32
BF16 = jnp.bfloat16


def noise_table():
    levels = np.arange(TRAIN_STEPS, dtype=np.float32)
    beta = (0.0001 + (0.02 - 0.0001) * levels / (TRAIN_STEPS - 1)).astype(np.float32)
    bars = np.exp(np.cumsum(np.log1p(-beta.astype(np.float64)))).astype(np.float32)
    padded = np.zeros((-(-TRAIN_STEPS // (8 * LANES)) * 8 * LANES,), np.float32)
    padded[:TRAIN_STEPS] = bars
    return padded.reshape(-1, LANES)


def frequencies(count):
    powers = -math.log(10000.0) * np.arange(count, dtype=np.float32) / count
    return np.exp(powers.astype(np.float32)).astype(np.float32)[None, :]


def group_matrix(channels, rows):
    width = channels // GROUPS
    place = np.arange(BLOCK) // width
    same = (place[:, None] == place[None, :]).astype(np.float32)
    return same / (width * rows)


def silu_of_half(half):
    return half + half * jnp.tanh(half)


def kernel(
    cfg,
    gap_hbm,
    start_level_hbm,
    table_hbm,
    freq_hbm,
    group_hbm,
    start_hbm,
    noise_hbm,
    win_hbm,
    wemb_hbm,
    w1_hbm,
    w2_hbm,
    wout_hbm,
    out_v,
    gap_ref,
    start_level_ref,
    table_ref,
    freq_ref,
    group_ref,
    start_v,
    noise_v,
    noise_all,
    win,
    wemb,
    w1,
    w2,
    wout,
    gap_send,
    gap_all,
    base_rx,
    base_tx,
    modulation_v,
    coef_v,
    part_v,
    state_v,
    chain_rx,
    chain_tx,
    out_tx,
    eps_v,
    load_sem,
    gap_send_sem,
    gap_recv_sem,
    base_sem,
    noise_send,
    noise_recv,
    chain_send,
    chain_recv,
    out_send,
    out_recv,
):
    steps, inner, columns, own, patches, features, channels = cfg
    rows = steps // columns
    plane = columns * inner
    s = lax.axis_index("steps")
    h = lax.axis_index("inner")
    z = s // columns
    p = lax.rem(s, columns) * inner + h
    first = p * own

    def load(i, src, dst):
        return pltpu.make_async_copy(src, dst, load_sem.at[i])

    loads = [
        load(0, noise_hbm, noise_v),
        load(1, start_hbm.at[pl.ds(first, own)], start_v),
        load(2, win_hbm, win),
        load(3, noise_hbm.at[pl.ds(first, own)], noise_all.at[p]),
        load(4, wemb_hbm, wemb),
        load(5, w1_hbm, w1),
        load(6, w2_hbm, w2),
        load(7, wout_hbm, wout),
        load(8, gap_hbm, gap_ref),
        load(9, start_level_hbm, start_level_ref),
        load(10, table_hbm, table_ref),
        load(11, freq_hbm, freq_ref),
        load(12, group_hbm, group_ref),
    ]
    def mate(r):
        q = lax.rem(p + r, plane)
        return q, {"steps": z * columns + q // inner, "inner": lax.rem(q, inner)}

    below, above = {"steps": s - columns}, {"steps": s + columns}

    barrier = pltpu.get_barrier_semaphore()
    for r in range(1, plane):
        pl.semaphore_signal(barrier, inc=1, device_id=mate(r)[1], device_id_type=MESH)

    @pl.when(z > 0)
    def _():
        pl.semaphore_signal(barrier, inc=1, device_id=below, device_id_type=MESH)

    @pl.when(z < rows - 1)
    def _():
        pl.semaphore_signal(barrier, inc=1, device_id=above, device_id_type=MESH)

    for i in (8, 0, 9, 10, 11, 1, 2, 12, 3, 4, 5, 6, 7):
        loads[i].start()

    loads[8].wait()
    gap_send[...] = jnp.zeros_like(gap_send) + gap_ref[0]
    gap_all[p] = jnp.zeros_like(gap_send) + gap_ref[0]

    @pl.when(z == 0)
    def _():
        base_rx[...] = jnp.zeros_like(base_rx)
        chain_rx[...] = jnp.zeros_like(chain_rx)

    neighbours = (z + rows - 1) // rows + (2 * rows - 2 - z) // rows
    pl.semaphore_wait(barrier, plane - 1 + neighbours)

    def gap_copy(r, slot):
        return pltpu.make_async_remote_copy(
            src_ref=gap_send,
            dst_ref=gap_all.at[slot],
            send_sem=gap_send_sem.at[r],
            recv_sem=gap_recv_sem.at[slot],
            device_id=mate(r)[1],
            device_id_type=MESH,
        )

    def base_copy():
        return pltpu.make_async_remote_copy(
            src_ref=base_tx,
            dst_ref=base_rx,
            send_sem=base_sem.at[0],
            recv_sem=base_sem.at[1],
            device_id=above,
            device_id_type=MESH,
        )

    def noise_copy(j, r, slot):
        q, device = mate(r)
        return pltpu.make_async_remote_copy(
            src_ref=noise_v.at[q * own + j],
            dst_ref=noise_all.at[slot, j],
            send_sem=noise_send.at[j, r],
            recv_sem=noise_recv.at[slot, j],
            device_id=device,
            device_id_type=MESH,
        )

    depth = patches // PIECES

    def out_copy(j, r, slot, piece):
        q, device = mate(r)
        cut = pl.ds(piece * depth, depth)
        return pltpu.make_async_remote_copy(
            src_ref=out_tx.at[j, q, cut],
            dst_ref=out_v.at[slot * own + j, cut],
            send_sem=out_send.at[j, r, piece],
            recv_sem=out_recv.at[slot, j, piece],
            device_id=device,
            device_id_type=MESH,
        )

    def chain_copy(n, j, q):
        cut = pl.ds(q * depth, depth)
        return pltpu.make_async_remote_copy(
            src_ref=chain_tx.at[n, j, cut],
            dst_ref=chain_rx.at[n, j, cut],
            send_sem=chain_send.at[n, j, q],
            recv_sem=chain_recv.at[n, j, q],
            device_id=above,
            device_id_type=MESH,
        )

    for r in range(1, plane):
        gap_copy(r, p).start()
    loads[0].wait()
    for j in range(own):
        for r in range(1, plane):
            noise_copy(j, r, p).start()

    def cut_columns(value):
        return [value[..., i : i + BLOCK] for i in range(0, value.shape[-1], BLOCK)]

    def pack(partial):
        row = lax.broadcasted_iota(jnp.int32, (8, BLOCK), 0)
        top, late = row < 4, lax.rem(row, 4) >= 2
        packed = []
        for i in range(0, partial.shape[0], 4):
            a, b, c, d = (partial[i + k] for k in range(4))
            ab = jnp.where(top, a, b) + pltpu.roll(jnp.where(top, b, a), 4, 0)
            cd = jnp.where(top, c, d) + pltpu.roll(jnp.where(top, d, c), 4, 0)
            four = jnp.where(late, ab + pltpu.roll(ab, 2, 0), cd + pltpu.roll(cd, 6, 0))
            packed.append(four + pltpu.roll(four, 1, 0))
        return packed

    def group_averages(partials):
        size = partials[0].shape[0]
        whole = size % 4 == 0
        rows = []
        for partial in partials:
            rows.extend(pack(partial) if whole else [partial.reshape(size * 8, BLOCK)])
        rows = jnp.concatenate(rows, axis=0)
        high = rows.astype(BF16).astype(F32)
        rest = rows - high
        middle = rest.astype(BF16).astype(F32)
        parts = jnp.concatenate([rest - middle, middle, high], axis=0).astype(BF16)
        summed = jnp.dot(parts, group_ref[...], preferred_element_type=F32)
        summed = jnp.sum(summed.reshape(3, len(partials), -1, BLOCK), axis=0)
        if not whole:
            summed = summed.reshape(len(partials), size, 8, BLOCK)
            return list(jnp.sum(summed, axis=2, keepdims=True))
        places = [i // 4 * 8 + (3, 7, 1, 5)[i % 4] for i in range(size)]
        return [jnp.stack([block[r : r + 1] for r in places], axis=0) for block in summed]

    def row_sums(value):
        size = value.shape[0]
        return jnp.sum(value.reshape(size, patches // 8, 8, BLOCK), axis=1)

    def pivots(block):
        rows = block[:, 0, :]
        lane = lax.broadcasted_iota(jnp.int32, (rows.shape[0], LANES), 1)
        lead = lane - lax.rem(lane, channels // GROUPS)
        halves = [
            jnp.take_along_axis(rows[:, i : i + LANES], lead, axis=1)
            for i in range(0, BLOCK, LANES)
        ]
        return jnp.concatenate(halves, axis=1)[:, None, :]

    def centered(block):
        shifted = block - pivots(block)
        mean, square = group_averages([row_sums(shifted), row_sums(shifted * shifted)])
        return shifted, mean, lax.rsqrt(jnp.maximum(square - mean * mean, 0.0) + 1e-05)

    def project(acts, weight, outer=True):
        sums = [None] * (weight.shape[1] // BLOCK)
        pairs = [(k, n) for k in range(len(acts)) for n in range(len(sums))]
        if not outer:
            pairs = [(k, n) for n in range(len(sums)) for k in range(len(acts))]
        for k, n in pairs:
            tile = weight[pl.ds(k * BLOCK, BLOCK), pl.ds(n * BLOCK, BLOCK)]
            part = jnp.dot(acts[k], tile, preferred_element_type=F32)
            sums[n] = part if sums[n] is None else sums[n] + part
        return sums

    def shape_images(blocks, size):
        return [block.reshape(size, patches, BLOCK) for block in blocks]

    def flatten(value):
        return value.reshape(-1, BLOCK).astype(BF16)

    def activate(blocks):
        result = []
        for block in blocks:
            shifted, mean, spread = centered(block)
            gain = 0.5 * spread
            result.append(flatten(silu_of_half(shifted * gain - mean * gain)))
        return result

    def set_levels():
        for r in range(1, plane):
            slot = mate(r)[0]
            gap_copy(r, slot).wait_recv()

        @pl.when(z > 0)
        def _():
            base_copy().wait_recv()

        gaps = [gap_all[t] for t in range(plane)]
        base = base_rx[...]
        total = base
        for gap in gaps:
            total = total + gap
        base_tx[...] = total

        @pl.when(z < rows - 1)
        def _():
            base_copy().start()

        for i in (9, 10, 11):
            loads[i].wait()
        table = table_ref[...]
        tall = lax.broadcasted_iota(jnp.int32, table.shape, 0)
        places = tall * LANES + lax.broadcasted_iota(jnp.int32, table.shape, 1)
        level = start_level_ref[0] - base
        levels = [level]
        for gap in gaps:
            level = level - gap
            levels.append(level)

        def lookup(level):
            found = jnp.where(places == level[:1, :1], table, 0.0)
            return jnp.sum(jnp.sum(found, axis=0, keepdims=True), axis=1, keepdims=True)

        bars = [lookup(level) for level in levels]
        bar_now, bar_next = jnp.ones(table.shape, F32), jnp.ones(table.shape, F32)
        level_now = levels[0]
        for t in range(plane):
            bar_now = jnp.where(tall == t, bars[t], bar_now)
            bar_next = jnp.where(tall == t, bars[t + 1], bar_next)
            level_now = jnp.where(tall == t, levels[t], level_now)
        rest = 1.0 - bar_now
        lift = (1.0 - bar_next) * jnp.sqrt(bar_now / (bar_next * rest)) / jnp.sqrt(rest)
        coefs = [
            1.0 / jnp.sqrt(bar_now),
            jnp.sqrt(rest) / jnp.sqrt(bar_now),
            jnp.sqrt(bar_next) - lift * jnp.sqrt(bar_now),
            lift - 1.0,
            jnp.sqrt((1.0 - bar_next) / rest * (1.0 - bar_now / bar_next)),
        ]
        for i, coef in enumerate(coefs):
            coef_v[i] = coef
        angles = level_now.astype(F32) * freq_ref[...]
        around = jnp.concatenate([jnp.cos(angles), jnp.sin(angles)], axis=1).astype(BF16)
        loads[4].wait()
        modulation_v[...] = jnp.dot(around, wemb[...], preferred_element_type=F32)

    def modulations(low):
        cut = pl.ds(low, BLOCK)
        return jnp.concatenate(
            [modulation_v[t : t + 1, cut] for t in range(plane)], axis=0
        ).reshape(plane, 1, BLOCK)

    def drifts(n, j, eps):
        result = []
        for t in range(plane):
            state = start_v[j] if n == 0 else state_v[j, t]
            coef = [coef_v[i][t : t + 1, :1] for i in range(5)]
            clean = jnp.clip(state * coef[0] - eps[t] * coef[1], -1.0, 1.0)
            result.append(coef[2] * clean + coef[3] * state + coef[4] * noise_all[t, j])
        return result

    def launch(n, j):
        @pl.when(z == 0)
        def _():
            for q in range(PIECES):
                chain_copy(n, j, q).start()

    def forward(n, j, q):
        @pl.when(z > 0)
        def _():
            cut = pl.ds(q * depth, depth)
            chain_copy(n, j, q).wait_recv()
            chain_tx[n, j, cut] = chain_tx[n, j, cut] + chain_rx[n, j, cut]

            @pl.when(z < rows - 1)
            def _():
                chain_copy(n, j, q).start()

    def denoise(entries, norms, hook, outer):
        images, times = entries[0].shape[:2]
        count = images * plane
        ones = []
        for i, (shifted, mean, spread) in enumerate(norms):
            scale, shift = modulations(i * BLOCK), modulations(channels + i * BLOCK)
            gain = spread * (0.5 + 0.5 * scale[None])
            ones.append(flatten(silu_of_half(shifted * gain + (0.5 * shift[None] - mean * gain))))
        hook(0)
        twos = activate(shape_images(project(ones, w1, outer), count))
        hook(1)
        blocks = []
        for entry, extra in zip(entries, project(twos, w2, outer)):
            total = entry + extra.reshape(images, plane, patches, BLOCK)
            blocks.append(total.reshape(count, patches, BLOCK))
        threes = activate(blocks)
        hook(2)
        eps = jnp.concatenate(project(threes, wout, outer), axis=1)
        hook(3)
        return eps.reshape(images, plane, patches, features)

    def entrance(flat, images, times, outer):
        count = images * times
        blocks = shape_images(project(cut_columns(flat), win, outer), count)
        entries = [block.reshape(images, times, patches, BLOCK) for block in blocks]
        norms = []
        for block in blocks:
            shifted, mean, spread = centered(block)
            stats = (value.reshape(images, times, 1, BLOCK) for value in (mean, spread))
            norms.append((shifted.reshape(images, times, patches, BLOCK), *stats))
        return entries, norms

    def finish_first(j, eps):
        if j == 0:
            loads[3].wait()
        for r in range(1, plane):
            slot = mate(r)[0]
            noise_copy(j, r, slot).wait_recv()
        parts = drifts(0, j, eps)
        running = parts[0]
        for t in range(1, plane):
            part_v[j, t] = running
            running = running + parts[t]
        chain_tx[0, j] = running
        launch(0, j)

    def second(j, hook):
        state_v[j, 0] = start_v[j] + chain_rx[0, j]
        for t in range(1, plane):
            state_v[j, t] = start_v[j] + (chain_rx[0, j] + part_v[j, t])
        flat = state_v[j].reshape(plane * patches, features).astype(BF16)
        eps = denoise(*entrance(flat, 1, plane, OUTER_TWO), hook, OUTER_TWO)[0]
        parts = drifts(1, j, eps)
        running = parts[0]
        origin = start_v[j]
        out_tx[j, 0] = origin + running
        for t in range(1, plane):
            running = running + parts[t]
            out_tx[j, t] = origin + running
        chain_tx[1, j] = running
        launch(1, j)
        for q in range(PIECES):
            forward(1, j, q)
            cut = pl.ds(q * depth, depth)
            for t in range(plane):
                out_tx[j, t, cut] = out_tx[j, t, cut] + chain_rx[1, j, cut]
            for r in range(1, plane):
                out_copy(j, r, p, q).start()
        out_v[first + j] = out_tx[j, p]

    for i in (1, 2, 12):
        loads[i].wait()
    flat = start_v[...].reshape(own * patches, features).astype(BF16)
    entries, norms = entrance(flat, own, 1, OUTER_ONE)
    for i in (5, 6, 7):
        loads[i].wait()
    set_levels()

    def idle(stage):
        pass

    eps = denoise(entries, norms, idle, OUTER_ONE)
    for j in range(1, own):
        eps_v[j - 1] = eps[j]
    finish_first(0, eps[0])

    for j in range(1, own):

        def relay(stage):
            if stage == 2:
                forward(0, j, 0)
            if stage == 3:
                for q in range(1, PIECES // 2 + 1):
                    forward(0, j, q)

        if j == 1:
            for q in range(PIECES):
                forward(0, 0, q)

        @pl.when(z > 0)
        def _():
            finish_first(j, eps_v[j - 1])

        second(j - 1, relay)

        @pl.when(z == 0)
        def _():
            finish_first(j, eps_v[j - 1])

        for q in range(PIECES // 2 + 1, PIECES):
            forward(0, j, q)

    second(own - 1, idle)

    for r in range(1, plane):
        slot = mate(r)[0]
        for j in range(own):
            for q in range(PIECES):
                out_copy(j, r, slot, q).wait_recv()

    for r in range(1, plane):
        gap_copy(r, p).wait_send()
        for j in range(own):
            noise_copy(j, r, p).wait_send()
            for q in range(PIECES):
                out_copy(j, r, p, q).wait_send()

    @pl.when(z < rows - 1)
    def _():
        base_copy().wait_send()
        for n in range(ITERS):
            for j in range(own):
                for q in range(PIECES):
                    chain_copy(n, j, q).wait_send()


def shards(
    steps,
    inner,
    start_state,
    noise_draws,
    step_gaps,
    window_start,
    input_weight,
    embed_weight,
    first_weight,
    second_weight,
    output_weight,
):
    batch, patches, features = start_state.shape
    channels = input_weight.shape[1]
    columns = 2 if steps % 2 == 0 else 1
    plane = columns * inner
    own = batch // plane
    cfg = (steps, inner, columns, own, patches, features, channels)
    image = (patches, features)
    table = jnp.asarray(noise_table())
    freq = jnp.asarray(frequencies(embed_weight.shape[0] // 2))
    matrix = jnp.asarray(group_matrix(channels, patches)).astype(BF16)
    vmem = pl.BlockSpec(memory_space=pltpu.VMEM)
    anywhere = pl.BlockSpec(memory_space=pltpu.HBM)
    dma = pltpu.SemaphoreType.DMA
    out = pl.pallas_call(
        functools.partial(kernel, cfg),
        out_shape=pltpu.VMEM((batch,) + image, F32),
        in_specs=[anywhere] * 12,
        out_specs=vmem,
        scratch_shapes=[
            pltpu.SMEM((1,), jnp.int32),
            pltpu.SMEM((1,), jnp.int32),
            pltpu.VMEM(table.shape, F32),
            pltpu.VMEM(freq.shape, F32),
            pltpu.VMEM(matrix.shape, BF16),
            pltpu.VMEM((own,) + image, F32),
            pltpu.VMEM((batch,) + image, F32),
            pltpu.VMEM((plane, own) + image, F32),
            pltpu.VMEM(input_weight.shape, BF16),
            pltpu.VMEM(embed_weight.shape, BF16),
            pltpu.VMEM(first_weight.shape, BF16),
            pltpu.VMEM(second_weight.shape, BF16),
            pltpu.VMEM(output_weight.shape, BF16),
            pltpu.VMEM((8, LANES), jnp.int32),
            pltpu.VMEM((plane, 8, LANES), jnp.int32),
            pltpu.VMEM((8, LANES), jnp.int32),
            pltpu.VMEM((8, LANES), jnp.int32),
            pltpu.VMEM((8, 2 * channels), F32),
            pltpu.VMEM((5, 8, LANES), F32),
            pltpu.VMEM((own, plane) + image, F32),
            pltpu.VMEM((own, plane) + image, F32),
            pltpu.VMEM((ITERS, own) + image, F32),
            pltpu.VMEM((ITERS, own) + image, F32),
            pltpu.VMEM((own, plane) + image, F32),
            pltpu.VMEM((max(own - 1, 1), plane) + image, F32),
            dma((13,)),
            dma((plane,)),
            dma((plane,)),
            dma((2,)),
            dma((own, plane)),
            dma((plane, own)),
            dma((ITERS, own, PIECES)),
            dma((ITERS, own, PIECES)),
            dma((own, plane, PIECES)),
            dma((plane, own, PIECES)),
        ],
        compiler_params=pltpu.CompilerParams(
            collective_id=0, has_side_effects=True, vmem_limit_bytes=56 * 1024 * 1024
        ),
    )(
        step_gaps,
        window_start,
        table,
        freq,
        matrix,
        start_state,
        noise_draws.reshape((batch,) + image),
        input_weight,
        embed_weight,
        first_weight,
        second_weight,
        output_weight,
    )
    return out.reshape((1,) + start_state.shape)


def solution(mesh):
    steps, inner = mesh.shape["steps"], mesh.shape["inner"]
    return jax.shard_map(
        functools.partial(shards, steps, inner),
        mesh=mesh,
        in_specs=(
            P("groups", None, None),
            P(("groups", "steps", "inner"), None, None, None),
            P(("groups", "steps", "inner")),
            P("groups"),
            P(),
            P(),
            P(),
            P(),
            P(),
        ),
        out_specs=P(("groups", "steps", "inner"), None, None, None),
        check_vma=False,
    )
```

time: 38 us -> 35.5 us (0.934)
  Pallas kernels: 35.7 us -> 33.1 us
    pallas_call x1, Pallas kernels: 35.7 us -> 33.1 us  [shards(): pl.pallas_call(functools.partial(kernel, cfg), out_shape=pltpu.VMEM((batc...]
where the time goes in v2:
time: 35.5 us; the launch traced here: 35.3 us
  Pallas kernels  33.1 us (93%)
  between operations  1.3 us (4%)
  local copies, waits for them, and re-layouts  0.88 us (2%)
    pallas_call x1, Pallas kernels, shards(): pl.pallas_call(functools.partial(kernel, cfg), out_shape=pltpu.VMEM((batc...  33.1 us
    unnamed x1, local copies, waits for them, and re-layouts  0.88 us

profile of v2, /device:TPU:25, one launch (start us, length us, event | category | flops | bytes accessed | tf_op | source)
XLA Modules:
  0.0 35.3 jit_solution(3126228088163896648)
XLA Ops:
  1.3 33.1 %shard_map.118 = f32[8,32,768]{2,1,0:T(8,128)S(1)} custom-call(s32[1]{0:T(128)S(6)} %copy.15.gap_hbm, s32[1]{0:T(128)S(6)} %copy.16.start_level_hbm, f32[8,128]{1,0:T(8,128)} %constant.6.clone.table_hbm, f32[1,128]{1,0:T(1,128)} %constant.7.clone.freq_hbm, bf16[256,256]{1,0:T(8,128)(2,1)} %constant.12.group_hbm, f32[8,32,768]{2,1,0:T(8,128)} %start_hbm.1, ...), custom_call_target="tpu_custom_call" | custom-call | tf_op jit(solution)/shard_map/pallas_call | solution.py:554
  34.4 0.9 %copy.14 = f32[1,8,32,768]{3,2,1,0:T(8,128)} copy(f32[1,8,32,768]{3,2,1,0:T(8,128)S(1)} %bitcast.2) | data formatting | bytes 1572864

commit v3 on v2

--- a/solution.py
+++ b/solution.py
@@ -87,6 +87,12 @@
     chain_tx,
     out_tx,
     eps_v,
+    pair_rx,
+    sum_tx,
+    sum_rx,
+    raw_tx,
+    raw_rx,
+    late_v,
     load_sem,
     gap_send_sem,
     gap_recv_sem,
@@ -97,6 +103,8 @@
     chain_recv,
     out_send,
     out_recv,
+    late_send,
+    late_recv,
 ):
     steps, inner, columns, own, patches, features, channels = cfg
     rows = steps // columns
@@ -104,8 +112,11 @@
     s = lax.axis_index("steps")
     h = lax.axis_index("inner")
     z = s // columns
-    p = lax.rem(s, columns) * inner + h
+    y = lax.rem(s, columns)
+    p = y * inner + h
     first = p * own
+    late = own - 1 if own > 1 and columns == 2 and inner == 2 else None
+    partner, across, other = p + 1 - 2 * h, (1 - y) * inner + h, (1 - y) * inner
 
     def load(i, src, dst):
         return pltpu.make_async_copy(src, dst, load_sem.at[i])
@@ -139,10 +150,6 @@
     def _():
         pl.semaphore_signal(barrier, inc=1, device_id=below, device_id_type=MESH)
 
-    @pl.when(z < rows - 1)
-    def _():
-        pl.semaphore_signal(barrier, inc=1, device_id=above, device_id_type=MESH)
-
     for i in (8, 0, 9, 10, 11, 1, 2, 12, 3, 4, 5, 6, 7):
         loads[i].start()
 
@@ -155,7 +162,7 @@
         base_rx[...] = jnp.zeros_like(base_rx)
         chain_rx[...] = jnp.zeros_like(chain_rx)
 
-    neighbours = (z + rows - 1) // rows + (2 * rows - 2 - z) // rows
+    neighbours = (2 * rows - 2 - z) // rows
     pl.semaphore_wait(barrier, plane - 1 + neighbours)
 
     def gap_copy(r, slot):
@@ -214,12 +221,36 @@
             device_id_type=MESH,
         )
 
+    def late_copy(i, src, dst, device):
+        return pltpu.make_async_remote_copy(
+            src_ref=src,
+            dst_ref=dst,
+            send_sem=late_send.at[i],
+            recv_sem=late_recv.at[i],
+            device_id=device,
+            device_id_type=MESH,
+        )
+
+    def late_move(i, slot):
+        beside, over = {"inner": 1 - h}, {"steps": z * columns + 1 - y}
+        if i == 0:
+            return late_copy(0, noise_v.at[(other + 1 - h) * own + late], pair_rx, beside)
+        if i == 1:
+            return late_copy(
+                1, noise_v.at[partner * own + late], noise_all.at[slot, late], beside
+            )
+        return late_copy(i, *((sum_tx, sum_rx) if i == 2 else (raw_tx, raw_rx)), over)
+
+    plain = [j for j in range(own) if j != late]
     for r in range(1, plane):
         gap_copy(r, p).start()
     loads[0].wait()
-    for j in range(own):
+    for j in plain:
         for r in range(1, plane):
             noise_copy(j, r, p).start()
+    if late is not None:
+        for i in (0, 1):
+            late_move(i, p).start()
 
     def cut_columns(value):
         return [value[..., i : i + BLOCK] for i in range(0, value.shape[-1], BLOCK)]
@@ -363,14 +394,32 @@
             [modulation_v[t : t + 1, cut] for t in range(plane)], axis=0
         ).reshape(plane, 1, BLOCK)
 
+    def noise_of(n, j, t):
+        if j != late:
+            return coef_v[4][t : t + 1, :1] * noise_all[t, j]
+        return late_v[t] if n else None
+
     def drifts(n, j, eps):
         result = []
         for t in range(plane):
             state = start_v[j] if n == 0 else state_v[j, t]
-            coef = [coef_v[i][t : t + 1, :1] for i in range(5)]
+            coef = [coef_v[i][t : t + 1, :1] for i in range(4)]
             clean = jnp.clip(state * coef[0] - eps[t] * coef[1], -1.0, 1.0)
-            result.append(coef[2] * clean + coef[3] * state + coef[4] * noise_all[t, j])
+            drift = coef[2] * clean + coef[3] * state
+            noise = noise_of(n, j, t)
+            result.append(drift if noise is None else drift + noise)
         return result
+
+    def weight(slot):
+        return coef_v[4, pl.ds(slot, 1), :1]
+
+    def blend():
+        late_move(0, p).wait_recv()
+        mine, theirs = noise_v[across * own + late], pair_rx[...]
+        sum_tx[...] = weight(p) * mine + weight(partner) * theirs
+        raw_tx[...] = jnp.where(h == 0, mine, theirs)
+        for i in (2, 3):
+            late_move(i, p).start()
 
     def launch(n, j):
         @pl.when(z == 0)
@@ -424,18 +473,38 @@
     def finish_first(j, eps):
         if j == 0:
             loads[3].wait()
-        for r in range(1, plane):
-            slot = mate(r)[0]
-            noise_copy(j, r, slot).wait_recv()
+        if j != late:
+            for r in range(1, plane):
+                slot = mate(r)[0]
+                noise_copy(j, r, slot).wait_recv()
         parts = drifts(0, j, eps)
         running = parts[0]
         for t in range(1, plane):
             part_v[j, t] = running
             running = running + parts[t]
+        if j == late:
+            for i in (1, 2):
+                late_move(i, partner).wait_recv()
+            near = y * inner
+            for i in range(inner):
+                late_v[near + i] = weight(near + i) * noise_all[near + i, late]
+            running = running + (late_v[near] + late_v[near + 1] + sum_rx[...])
         chain_tx[0, j] = running
         launch(0, j)
 
+    def finish_late():
+        late_move(3, partner).wait_recv()
+        lead = weight(other) * raw_rx[...]
+        late_v[other] = lead
+        late_v[other + 1] = sum_rx[...] - lead
+        running = late_v[0]
+        for t in range(1, plane):
+            part_v[late, t] = part_v[late, t] + running
+            running = running + late_v[t]
+
     def second(j, hook):
+        if j == late:
+            finish_late()
         state_v[j, 0] = start_v[j] + chain_rx[0, j]
         for t in range(1, plane):
             state_v[j, t] = start_v[j] + (chain_rx[0, j] + part_v[j, t])
@@ -470,35 +539,33 @@
     def idle(stage):
         pass
 
+    if late is not None:
+        blend()
     eps = denoise(entries, norms, idle, OUTER_ONE)
     for j in range(1, own):
         eps_v[j - 1] = eps[j]
     finish_first(0, eps[0])
 
+    for q in range(PIECES):
+        forward(0, 0, q)
     for j in range(1, own):
-
-        def relay(stage):
-            if stage == 2:
-                forward(0, j, 0)
-            if stage == 3:
-                for q in range(1, PIECES // 2 + 1):
-                    forward(0, j, q)
-
-        if j == 1:
-            for q in range(PIECES):
-                forward(0, 0, q)
 
         @pl.when(z > 0)
         def _():
             finish_first(j, eps_v[j - 1])
 
+        def relay(stage):
+            if stage == 2:
+
+                @pl.when(z == 0)
+                def _():
+                    finish_first(j, eps_v[j - 1])
+
+            if stage < PIECES:
+                forward(0, j, stage)
+
         second(j - 1, relay)
-
-        @pl.when(z == 0)
-        def _():
-            finish_first(j, eps_v[j - 1])
-
-        for q in range(PIECES // 2 + 1, PIECES):
+        for q in range(4, PIECES):
             forward(0, j, q)
 
     second(own - 1, idle)
@@ -511,10 +578,14 @@
 
     for r in range(1, plane):
         gap_copy(r, p).wait_send()
+        for j in plain:
+            noise_copy(j, r, p).wait_send()
         for j in range(own):
-            noise_copy(j, r, p).wait_send()
             for q in range(PIECES):
                 out_copy(j, r, p, q).wait_send()
+    if late is not None:
+        for i in range(4):
+            late_move(i, p).wait_send()
 
     @pl.when(z < rows - 1)
     def _():
@@ -582,6 +653,10 @@
             pltpu.VMEM((ITERS, own) + image, F32),
             pltpu.VMEM((own, plane) + image, F32),
             pltpu.VMEM((max(own - 1, 1), plane) + image, F32),
+        ]
+        + [pltpu.VMEM(image, F32)] * 5
+        + [
+            pltpu.VMEM((plane,) + image, F32),
             dma((13,)),
             dma((plane,)),
             dma((plane,)),
@@ -592,6 +667,8 @@
             dma((ITERS, own, PIECES)),
             dma((own, plane, PIECES)),
             dma((plane, own, PIECES)),
+            dma((4,)),
+            dma((4,)),
         ],
         compiler_params=pltpu.CompilerParams(
             collective_id=0, has_side_effects=True, vmem_limit_bytes=56 * 1024 * 1024

time: 35.5 us -> 33.5 us (0.944)
  Pallas kernels: 33.1 us -> 31.2 us
    pallas_call x1, Pallas kernels: 33.1 us -> 31.2 us  [shards(): pl.pallas_call(functools.partial(kernel, cfg), out_shape=pltpu.VMEM((batc...]
where the time goes in v3:
time: 33.5 us; the launch traced here: 33.4 us
  Pallas kernels  31.2 us (93%)
  between operations  1.3 us (4%)
  local copies, waits for them, and re-layouts  0.88 us (3%)
    pallas_call x1, Pallas kernels, shards(): pl.pallas_call(functools.partial(kernel, cfg), out_shape=pltpu.VMEM((batc...  31.2 us
    unnamed x1, local copies, waits for them, and re-layouts  0.88 us

profile of v3, /device:TPU:25, one launch (start us, length us, event | category | flops | bytes accessed | tf_op | source)
XLA Modules:
  0.0 33.4 jit_solution(11210639892042297616)
XLA Ops:
  1.3 31.2 %shard_map.118 = f32[8,32,768]{2,1,0:T(8,128)S(1)} custom-call(s32[1]{0:T(128)S(6)} %copy.15.gap_hbm, s32[1]{0:T(128)S(6)} %copy.16.start_level_hbm, f32[8,128]{1,0:T(8,128)} %constant.6.clone.table_hbm, f32[1,128]{1,0:T(1,128)} %constant.7.clone.freq_hbm, bf16[256,256]{1,0:T(8,128)(2,1)} %constant.12.group_hbm, f32[8,32,768]{2,1,0:T(8,128)} %start_hbm.1, ...), custom_call_target="tpu_custom_call" | custom-call | tf_op jit(solution)/shard_map/pallas_call | solution.py:625
  32.5 0.9 %copy.14 = f32[1,8,32,768]{3,2,1,0:T(8,128)} copy(f32[1,8,32,768]{3,2,1,0:T(8,128)S(1)} %bitcast.2) | data formatting | bytes 1572864

commit v4 on v3

--- a/solution.py
+++ b/solution.py
@@ -11,6 +11,8 @@
 
 GROUPS = 32
 PIECES = 4
+LATE_STAGE = 3
+RELAY = {1: (0, 1), 3: (2, 3)}
 OUTER_ONE = False
 OUTER_TWO = False
 ITERS = 2
@@ -49,8 +51,8 @@
 
 def kernel(
     cfg,
-    gap_hbm,
-    start_level_hbm,
+    gap_ref,
+    start_level_ref,
     table_hbm,
     freq_hbm,
     group_hbm,
@@ -62,8 +64,6 @@
     w2_hbm,
     wout_hbm,
     out_v,
-    gap_ref,
-    start_level_ref,
     table_ref,
     freq_ref,
     group_ref,
@@ -130,11 +130,9 @@
         load(5, w1_hbm, w1),
         load(6, w2_hbm, w2),
         load(7, wout_hbm, wout),
-        load(8, gap_hbm, gap_ref),
-        load(9, start_level_hbm, start_level_ref),
-        load(10, table_hbm, table_ref),
-        load(11, freq_hbm, freq_ref),
-        load(12, group_hbm, group_ref),
+        load(8, table_hbm, table_ref),
+        load(9, freq_hbm, freq_ref),
+        load(10, group_hbm, group_ref),
     ]
     def mate(r):
         q = lax.rem(p + r, plane)
@@ -150,10 +148,9 @@
     def _():
         pl.semaphore_signal(barrier, inc=1, device_id=below, device_id_type=MESH)
 
-    for i in (8, 0, 9, 10, 11, 1, 2, 12, 3, 4, 5, 6, 7):
+    for i in (0, 1, 2, 8, 9, 10, 3, 4, 5, 6, 7):
         loads[i].start()
 
-    loads[8].wait()
     gap_send[...] = jnp.zeros_like(gap_send) + gap_ref[0]
     gap_all[p] = jnp.zeros_like(gap_send) + gap_ref[0]
 
@@ -350,7 +347,7 @@
         def _():
             base_copy().start()
 
-        for i in (9, 10, 11):
+        for i in (8, 9):
             loads[i].wait()
         table = table_ref[...]
         tall = lax.broadcasted_iota(jnp.int32, table.shape, 0)
@@ -528,13 +525,13 @@
                 out_copy(j, r, p, q).start()
         out_v[first + j] = out_tx[j, p]
 
-    for i in (1, 2, 12):
+    for i in (1, 2, 10):
         loads[i].wait()
     flat = start_v[...].reshape(own * patches, features).astype(BF16)
     entries, norms = entrance(flat, own, 1, OUTER_ONE)
+    set_levels()
     for i in (5, 6, 7):
         loads[i].wait()
-    set_levels()
 
     def idle(stage):
         pass
@@ -555,18 +552,16 @@
             finish_first(j, eps_v[j - 1])
 
         def relay(stage):
-            if stage == 2:
+            if stage == LATE_STAGE:
 
                 @pl.when(z == 0)
                 def _():
                     finish_first(j, eps_v[j - 1])
 
-            if stage < PIECES:
-                forward(0, j, stage)
+            for q in RELAY.get(stage, ()):
+                forward(0, j, q)
 
         second(j - 1, relay)
-        for q in range(4, PIECES):
-            forward(0, j, q)
 
     second(own - 1, idle)
 
@@ -625,11 +620,9 @@
     out = pl.pallas_call(
         functools.partial(kernel, cfg),
         out_shape=pltpu.VMEM((batch,) + image, F32),
-        in_specs=[anywhere] * 12,
+        in_specs=[pl.BlockSpec(memory_space=pltpu.SMEM)] * 2 + [anywhere] * 10,
         out_specs=vmem,
         scratch_shapes=[
-            pltpu.SMEM((1,), jnp.int32),
-            pltpu.SMEM((1,), jnp.int32),
             pltpu.VMEM(table.shape, F32),
             pltpu.VMEM(freq.shape, F32),
             pltpu.VMEM(matrix.shape, BF16),
@@ -657,7 +650,7 @@
         + [pltpu.VMEM(image, F32)] * 5
         + [
             pltpu.VMEM((plane,) + image, F32),
-            dma((13,)),
+            dma((11,)),
             dma((plane,)),
             dma((plane,)),
             dma((2,)),

time: 33.5 us -> 33.6 us (level)
  no operation moved by 1% of the time
where the time goes in v4:
time: 33.6 us; the launch traced here: 33.4 us
  Pallas kernels  31.2 us (93%)
  between operations  1.3 us (4%)
  local copies, waits for them, and re-layouts  0.88 us (3%)
    pallas_call x1, Pallas kernels, shards(): pl.pallas_call(functools.partial(kernel, cfg), out_shape=pltpu.VMEM((batc...  31.2 us
    unnamed x1, local copies, waits for them, and re-layouts  0.88 us

profile of v4, /device:TPU:25, one launch (start us, length us, event | category | flops | bytes accessed | tf_op | source)
XLA Modules:
  0.0 33.4 jit_solution(15700913732354648914)
XLA Ops:
  1.3 31.2 %shard_map.118 = f32[8,32,768]{2,1,0:T(8,128)S(1)} custom-call(s32[1]{0:T(128)S(6)} %copy.15.gap_ref, s32[1]{0:T(128)S(6)} %copy.16.start_level_ref, f32[8,128]{1,0:T(8,128)} %constant.6.clone.table_hbm, f32[1,128]{1,0:T(1,128)} %constant.7.clone.freq_hbm, bf16[256,256]{1,0:T(8,128)(2,1)} %constant.12.group_hbm, f32[8,32,768]{2,1,0:T(8,128)} %start_hbm.1, ...), custom_call_target="tpu_custom_call" | custom-call | tf_op jit(solution)/shard_map/pallas_call | solution.py:620
  32.5 0.9 %copy.14 = f32[1,8,32,768]{3,2,1,0:T(8,128)} copy(f32[1,8,32,768]{3,2,1,0:T(8,128)S(1)} %bitcast.2) | data formatting | bytes 1572864

commit v5 on v3

--- a/solution.py
+++ b/solution.py
@@ -242,11 +242,12 @@
         return late_copy(i, *((sum_tx, sum_rx) if i == 2 else (raw_tx, raw_rx)), over)
 
     plain = [j for j in range(own) if j != late]
+    order = sorted(range(1, plane), key=lambda r: r % inner)
     for r in range(1, plane):
         gap_copy(r, p).start()
     loads[0].wait()
     for j in plain:
-        for r in range(1, plane):
+        for r in order:
             noise_copy(j, r, p).start()
     if late is not None:
         for i in (0, 1):
@@ -432,10 +433,10 @@
         def _():
             cut = pl.ds(q * depth, depth)
             chain_copy(n, j, q).wait_recv()
-            chain_tx[n, j, cut] = chain_tx[n, j, cut] + chain_rx[n, j, cut]
 
             @pl.when(z < rows - 1)
             def _():
+                chain_tx[n, j, cut] = chain_tx[n, j, cut] + chain_rx[n, j, cut]
                 chain_copy(n, j, q).start()
 
     def denoise(entries, norms, hook, outer):
@@ -524,7 +525,7 @@
             cut = pl.ds(q * depth, depth)
             for t in range(plane):
                 out_tx[j, t, cut] = out_tx[j, t, cut] + chain_rx[1, j, cut]
-            for r in range(1, plane):
+            for r in order:
                 out_copy(j, r, p, q).start()
         out_v[first + j] = out_tx[j, p]
 

time: 33.5 us -> 33.5 us (level)
  no operation moved by 1% of the time
where the time goes in v5:
time: 33.5 us; the launch traced here: 33.3 us
  Pallas kernels  31.1 us (93%)
  between operations  1.3 us (4%)
  local copies, waits for them, and re-layouts  0.88 us (3%)
    pallas_call x1, Pallas kernels, shards(): pl.pallas_call(functools.partial(kernel, cfg), out_shape=pltpu.VMEM((batc...  31.1 us
    unnamed x1, local copies, waits for them, and re-layouts  0.88 us

profile of v5, /device:TPU:25, one launch (start us, length us, event | category | flops | bytes accessed | tf_op | source)
XLA Modules:
  0.0 33.3 jit_solution(894037746867938831)
XLA Ops:
  1.3 31.1 %shard_map.118 = f32[8,32,768]{2,1,0:T(8,128)S(1)} custom-call(s32[1]{0:T(128)S(6)} %copy.15.gap_hbm, s32[1]{0:T(128)S(6)} %copy.16.start_level_hbm, f32[8,128]{1,0:T(8,128)} %constant.6.clone.table_hbm, f32[1,128]{1,0:T(1,128)} %constant.7.clone.freq_hbm, bf16[256,256]{1,0:T(8,128)(2,1)} %constant.12.group_hbm, f32[8,32,768]{2,1,0:T(8,128)} %start_hbm.1, ...), custom_call_target="tpu_custom_call" | custom-call | tf_op jit(solution)/shard_map/pallas_call | solution.py:626
  32.4 0.9 %copy.14 = f32[1,8,32,768]{3,2,1,0:T(8,128)} copy(f32[1,8,32,768]{3,2,1,0:T(8,128)S(1)} %bitcast.2) | data formatting | bytes 1572864
